TPU v7x, 256 devices: a whole 4x4x8 slice. The times are simulated.
256 devices in a mesh: nest: 4 (over y), tile: 64 (over z, x, core).
Axes of the slice: x: 4, y: 4, z: 8, core: 2. Of those that a mesh axis runs over, the one named last changes fastest.
Arguments:
- child_fields: float32 [4, 32, 1536, 3072], P('nest', None, 'tile'), may hold values from -18 to 18
- row_weights: float32 [8, 24], replicated
- col_weights: float32 [3072, 1024], replicated
- nest_offsets: int32 [4, 2], replicated, may hold values from 0 to 1023, as said below
- priority: int32 [1024, 1024], P('tile', 'nest'), may hold values from -1 to 3, as said below
- parent_old: float32 [32, 1024, 1024], P(None, 'tile', 'nest'), may hold values from -6 to 6
- smooth_rate: float32 [32], replicated, may hold values from 0.03 to 0.22
Outputs:
- parent_new: float32 [32, 1024, 1024], P(None, 'tile', 'nest')
Inputs may be any that keep to these rules, and one draw needn't show every extreme that they name: nest_offsets[n, 0] lies in 0 .. 512 and nest_offsets[n, 1] in 0 .. 1023. priority[x, y] is -1 or a nest n with nest_offsets[n, 0] <= y < nest_offsets[n, 0] + 512.
All inputs are finite; a program needn't handle non-finite values.
Results may differ from a plain program's by a relative error of at most 0.000058.
Values sent between devices are 32-bit elements; how exact they have to be, the bound alone decides.
A program may use at most 128 MiB of HBM per device.

v0:
```python
import jax
import jax.numpy as jnp
from jax import lax
from jax.sharding import PartitionSpec as P


def split_up(value, dim, count):
    lengths = value.shape
    blocks = value.reshape(*lengths[:dim], count, lengths[dim] // count, *lengths[dim + 1 :])
    return jnp.moveaxis(blocks, dim, 0)


def piece_ends(length, count):
    unit = 8 if length >= 8 * count else 1
    return [length // unit * k // count * unit for k in range(1, count)]


def laid_out(blocks, dim):
    lengths = list(blocks.shape[1:])
    lengths[dim] *= blocks.shape[0]
    return jnp.moveaxis(blocks, 0, dim).reshape(lengths)


def several_exchanges(value, axis, pieces, split_dim, concat_dim):
    blocks = split_up(value, split_dim, lax.axis_size(axis))
    split_at = max(range(1, max(2, blocks.ndim - 1)), key=lambda d: blocks.shape[d])
    done = []
    for piece in jnp.split(blocks, piece_ends(blocks.shape[split_at], pieces), axis=split_at):
        if piece.size:
            done.append(lax.all_to_all(piece, axis, split_axis=0, concat_axis=0, tiled=True))
    return laid_out(jnp.concatenate(done, axis=split_at), concat_dim)


def extended(value, sides, width):
    edges = {}
    for axis, dim in sides:
        count, length = (lax.axis_size(axis), value.shape[dim])
        up = [(i, (i + 1) % count) for i in range(count)]
        last = lax.slice_in_dim(value, length - width, length, axis=dim)
        leading = lax.slice_in_dim(value, 0, width, axis=dim)
        edges[dim] = (
            lax.ppermute(last, axis, up),
            lax.ppermute(leading, axis, [(b, a) for a, b in up]),
        )
    done = []
    for _, dim in sides:
        low, high = edges[dim]
        around = [(width, width) if d in done else (0, 0) for d in range(value.ndim)]
        value = jnp.concatenate([jnp.pad(low, around), value, jnp.pad(high, around)], axis=dim)
        done.append(dim)
    return value


def per_device(
    child_fields, row_weights, col_weights, nest_offsets, priority, parent_old, smooth_rate
):
    child_block = child_fields[0]
    planes = child_block.shape[0]
    cell_rows = row_weights.shape[0]
    tile_count = lax.axis_size("tile")
    nest_count = lax.axis_size("nest")
    strip_cols = parent_old.shape[1]
    owned_rows = parent_old.shape[2]
    nrows = cell_rows * tile_count
    nest_id = lax.axis_index("nest")
    thinned = jnp.einsum("pr,frc->fpc", row_weights, child_block, precision=lax.Precision.HIGHEST)
    restricted = jnp.einsum("fpc,cx->xfp", thinned, col_weights, precision=lax.Precision.HIGHEST)
    rolled = jnp.roll(restricted, nest_offsets[nest_id, 1], axis=0)
    outgoing = rolled.reshape(rolled.shape[0], planes * cell_rows)
    arrived = lax.all_to_all(outgoing, "tile", split_axis=0, concat_axis=0, tiled=True)
    column_slab = arrived.reshape(tile_count, strip_cols, planes, cell_rows)
    column_slab = column_slab.transpose(2, 1, 0, 3).reshape(planes, strip_cols, nrows)
    framed = jnp.zeros((planes, strip_cols, owned_rows * nest_count), jnp.float32)
    placed = lax.dynamic_update_slice(
        framed, column_slab, (jnp.int32(0), jnp.int32(0), nest_offsets[nest_id, 0])
    )
    received = several_exchanges(placed[None], "nest", 2, 3, 0)
    merged = parent_old
    for nest_num in range(nest_count):
        merged = jnp.where((priority == nest_num)[None], received[nest_num], merged)
    padded = extended(merged, (("nest", 2), ("tile", 1)), 1)
    west_side = padded[:, :-2, 1:-1]
    east_side = padded[:, 2:, 1:-1]
    south_side = padded[:, 1:-1, :-2]
    north_side = padded[:, 1:-1, 2:]
    south_side = jnp.where(
        nest_id == 0, jnp.concatenate([merged[:, :, :1], south_side[:, :, 1:]], axis=2), south_side
    )
    north_side = jnp.where(
        nest_id == nest_count - 1,
        jnp.concatenate([north_side[:, :, :-1], merged[:, :, -1:]], axis=2),
        north_side,
    )
    return merged + smooth_rate[:, None, None] * (
        east_side + west_side + north_side + south_side - 4.0 * merged
    )


def solution(mesh):
    return jax.shard_map(
        per_device,
        mesh=mesh,
        in_specs=(
            P("nest", None, "tile", None),
            P(),
            P(),
            P(),
            P("tile", "nest"),
            P(None, "tile", "nest"),
            P(),
        ),
        out_specs=P(None, "tile", "nest"),
        check_vma=False,
    )
```

profile of v0, /device:TPU:8, one launch (start us, length us, event | category | flops | bytes accessed | tf_op | source)
XLA Modules:
  0.0 144.5 jit_solution(4163988800008172533)
XLA Ops:
  0.0 0.0 copy-start
  0.0 1.4 constant_dynamic-slice_fusion
  3.5 0.0 copy-done
  3.5 0.0 copy-start.1
  3.5 8.1 %fusion.4 = f32[32,8,3072]{2,1,0:T(8,128)S(1)} fusion(f32[1,32,24,3072]{3,2,1,0:T(8,128)} %param.7, f32[8,24]{1,0:T(8,128)S(1)} %copy-done), kind=kOutput, calls=%fused_computation.4 | convolution fusion | flops 226492416 | bytes 12583680 | tf_op jit(solution)/shard_map/pr,frc->fpc/dot_general | solution.py:66
  11.7 0.0 copy-done.1
  11.7 11.2 %fusion.7 = f32[1024,32,8]{0,2,1:T(8,128)S(1)} fusion(f32[32,8,3072]{2,1,0:T(8,128)S(1)} %fusion.4, f32[3072,1024]{1,0:T(8,128)S(1)} %copy-done.1), kind=kOutput, calls=%fused_computation.7 | convolution fusion | flops 9663676416 | bytes 16777216 | tf_op jit(solution)/shard_map/fpc,cx->xfp/dot_general | solution.py:67
  22.9 0.6 fusion.10
  23.6 4.9 %all_to_all.12 = f32[64,16,256]{1,0,2:T(8,128)} reshape(f32[1024,32,8]{0,2,1:T(8,128)S(1)} %fusion.10) | data formatting | bytes 2097152 | tf_op jit(solution)/shard_map/all_to_all | solution.py:70
  28.4 7.1 %copy.18 = f32[64,16,256]{2,1,0:T(8,128)} copy(f32[64,16,256]{1,0,2:T(8,128)} %all_to_all.12) | data formatting | bytes 2097152 | tf_op jit(solution)/shard_map/all_to_all | solution.py:70
  35.5 12.1 %all-to-all-start = ((f32[64,16,256]{2,1,0:T(8,128)}), f32[64,16,256]{2,1,0:T(8,128)S(1)}, u32[]{:S(2)}, u32[]{:S(2)}) async-start(f32[64,16,256]{2,1,0:T(8,128)} %copy.18), calls=%async_computation | async-start | bytes 2097152 | tf_op jit(solution)/shard_map/all_to_all | solution.py:70
  49.6 26.7 %all-to-all-done = f32[64,16,256]{2,1,0:T(8,128)S(1)} async-done(((f32[64,16,256]{2,1,0:T(8,128)}), f32[64,16,256]{2,1,0:T(8,128)S(1)}, u32[]{:S(2)}, u32[]{:S(2)}) %all-to-all-start) | async-done | bytes 1048608 | tf_op jit(solution)/shard_map/all_to_all | solution.py:70
  76.3 0.7 copy.19
  77.1 2.7 %copy.20 = f32[32,16,64,8]{0,3,2,1:T(8,128)} copy(f32[32,16,64,8]{2,3,0,1:T(8,128)S(1)} %bitcast.50) | data formatting | bytes 2097152 | tf_op jit(solution)/shard_map/transpose | solution.py:72
  79.8 3.0 %copy.21 = f32[32,16,512]{2,1,0:T(8,128)S(1)} copy(f32[32,16,512]{0,2,1:T(8,128)} %bitcast.49) | data formatting | bytes 2097152 | tf_op jit(solution)/shard_map/reshape | solution.py:72
  82.8 0.2 broadcast_in_dim.32
  83.1 6.7 %dynamic_update_slice.3 = f32[32,16,1024]{2,1,0:T(8,128)S(1)} dynamic-update-slice(f32[32,16,1024]{2,1,0:T(8,128)S(1)} %broadcast_in_dim.32, f32[32,16,512]{2,1,0:T(8,128)S(1)} %copy.21, s32[]{:T(128)} %constant.39.clone.1, s32[]{:T(128)} %constant.39.clone.1, s32[]{:T(128)S(6)} %select_n.50) | dynamic-update-slice | bytes 2097156 | tf_op jit(solution)/shard_map/dynamic_update_slice | solution.py:74
  89.8 2.0 %reshape_broadcast_in_dim.3 = f32[1,32,16,4,256]{4,3,2,1,0:T(4,128)} reshape(f32[32,16,1024]{2,1,0:T(8,128)S(1)} %dynamic_update_slice.3) | data formatting | bytes 4194304 | tf_op jit(solution)/shard_map/reshape;broadcast_in_dim | solution.py:9
  91.8 1.9 %fusion.26 = (f32[4,1,16,16,256]{4,0,3,2,1:T(4,128)S(1)}, f32[4,1,16,16,256]{4,0,3,2,1:T(4,128)S(1)}) fusion(f32[4,1,32,16,256]{4,0,3,2,1:T(4,128)} %bitcast.51), kind=kLoop, calls=%fused_computation.46 | loop fusion | bytes 4194304 | tf_op jit(solution)/shard_map/split | solution.py:28
  93.7 1.2 copy.22
  94.9 0.0 copy-start.2
  94.9 5.1 %all-to-all-start.1 = ((f32[4,1,16,16,256]{4,3,2,1,0:T(8,128)}), f32[4,1,16,16,256]{4,3,2,1,0:T(8,128)S(1)}, u32[]{:S(2)}, u32[]{:S(2)}) async-start(f32[4,1,16,16,256]{4,3,2,1,0:T(8,128)} %copy.22), calls=%async_computation.1 | async-start | bytes 2097152 | tf_op jit(solution)/shard_map/all_to_all | solution.py:30
  100.0 1.2 copy.23
  101.2 12.0 %all-to-all-done.1 = f32[4,1,16,16,256]{4,3,2,1,0:T(8,128)S(1)} async-done(((f32[4,1,16,16,256]{4,3,2,1,0:T(8,128)}), f32[4,1,16,16,256]{4,3,2,1,0:T(8,128)S(1)}, u32[]{:S(2)}, u32[]{:S(2)}) %all-to-all-start.1) | async-done | bytes 1048608 | tf_op jit(solution)/shard_map/all_to_all | solution.py:30
  113.2 5.7 %all-to-all-start.2 = ((f32[4,1,16,16,256]{4,3,2,1,0:T(8,128)}), f32[4,1,16,16,256]{4,3,2,1,0:T(8,128)}, u32[]{:S(2)}, u32[]{:S(2)}) async-start(f32[4,1,16,16,256]{4,3,2,1,0:T(8,128)} %copy.23), calls=%async_computation.2 | async-start | bytes 2097152 | tf_op jit(solution)/shard_map/all_to_all | solution.py:30
  118.8 0.0 copy-done.2
  118.9 0.1 constant_dynamic-update-slice_fusion.1
  118.9 12.3 %all-to-all-done.2 = f32[4,1,16,16,256]{4,3,2,1,0:T(8,128)} async-done(((f32[4,1,16,16,256]{4,3,2,1,0:T(8,128)}), f32[4,1,16,16,256]{4,3,2,1,0:T(8,128)}, u32[]{:S(2)}, u32[]{:S(2)}) %all-to-all-start.2) | async-done | bytes 1048608 | tf_op jit(solution)/shard_map/all_to_all | solution.py:30
  131.3 1.3 constant_dynamic-update-slice_fusion
  132.6 0.0 copy-start.3
  132.6 1.4 fusion.24
  133.9 0.1 fusion.29
  134.1 0.1 collective-permute-start
  134.2 2.0 %collective-permute-start.1 = (f32[32,16,1]{2,1,0:T(8,128)S(1)}, f32[32,16,1]{2,1,0:T(8,128)S(1)}, u32[]{:S(2)}, u32[]{:S(2)}) collective-permute-start(f32[32,16,1]{2,1,0:T(8,128)S(1)} %get-tuple-element.11), channel_id=1, source_target_pairs={{64,0},{128,64},{192,128},{0,192},{65,1},{129,65},{193,129},{1,193... | collective-permute-start | bytes 6152 | tf_op jit(solution)/shard_map/ppermute | solution.py:43
  136.2 0.0 collective-permute-start.2
  136.3 0.5 collective-permute-start.3
  136.7 0.2 fusion.27
  136.9 3.6 %collective-permute-done = f32[32,16,1]{2,1,0:T(8,128)S(1)} collective-permute-done((f32[32,16,1]{2,1,0:T(8,128)S(1)}, f32[32,16,1]{2,1,0:T(8,128)S(1)}, u32[]{:S(2)}, u32[]{:S(2)}) %collective-permute-start) | collective-permute-done | bytes 2080 | tf_op jit(solution)/shard_map/ppermute | solution.py:42
  140.6 0.1 collective-permute-done.1
  140.7 0.0 collective-permute-done.2
  140.7 2.3 %collective-permute-done.3 = f32[32,1,256]{2,1,0:T(1,128)S(1)} collective-permute-done((f32[32,1,256]{2,1,0:T(1,128)S(1)}, f32[32,1,256]{2,1,0:T(1,128)S(1)}, u32[]{:S(2)}, u32[]{:S(2)}) %collective-permute-start.3) | collective-permute-done | bytes 32800 | tf_op jit(solution)/shard_map/ppermute | solution.py:42
  142.9 0.0 copy-done.3
  142.9 1.6 %fusion.15 = f32[32,16,256]{2,1,0:T(8,128)} fusion(f32[32,16,256]{2,1,0:T(8,128)S(1)} %fusion.24, f32[32,16,1]{2,1,0:T(8,128)S(1)} %collective-permute-done, f32[32,16,1]{2,1,0:T(8,128)S(1)} %collective-permute-done.1, f32[32,1,256]{2,1,0:T(1,128)S(1)} %collective-permute-done.3, f32[32,1,256]{2,1,0:T(1,128)S(1)} %collective-permute-done.2, ...), kind=kLoop, calls=%fused_computation.14 | loop fusion | flops 3276800 | bytes 2166914 | tf_op jit(solution)/shard_map/add | solution.py:94
  (2 shorter events, 0.1 us)
Async XLA Ops:
  0.0 3.5 %copy-start = (f32[8,24]{1,0:T(8,128)S(1)}, f32[8,24]{1,0:T(8,128)}, u32[]{:S(2)}) copy-start(f32[8,24]{1,0:T(8,128)} %param.8) | copy-start | bytes 2308
  3.5 8.1 %copy-start.1 = (f32[3072,1024]{1,0:T(8,128)S(1)}, f32[3072,1024]{1,0:T(8,128)}, u32[]{:S(2)}) copy-start(f32[3072,1024]{1,0:T(8,128)} %param.9) | copy-start | bytes 37748740
  35.5 40.8 %all-to-all-start = ((f32[64,16,256]{2,1,0:T(8,128)}), f32[64,16,256]{2,1,0:T(8,128)S(1)}, u32[]{:S(2)}, u32[]{:S(2)}) async-start(f32[64,16,256]{2,1,0:T(8,128)} %copy.18), calls=%async_computation | async-start | bytes 2097152 | tf_op jit(solution)/shard_map/all_to_all | solution.py:70
  94.9 23.9 %copy-start.2 = (s32[16,256]{1,0:T(8,128)S(1)}, s32[16,256]{1,0:T(8,128)}, u32[]{:S(2)}) copy-start(s32[16,256]{1,0:T(8,128)} %param.11) | copy-start | bytes 49156
  94.9 18.2 %all-to-all-start.1 = ((f32[4,1,16,16,256]{4,3,2,1,0:T(8,128)}), f32[4,1,16,16,256]{4,3,2,1,0:T(8,128)S(1)}, u32[]{:S(2)}, u32[]{:S(2)}) async-start(f32[4,1,16,16,256]{4,3,2,1,0:T(8,128)} %copy.22), calls=%async_computation.1 | async-start | bytes 2097152 | tf_op jit(solution)/shard_map/all_to_all | solution.py:30
  113.2 18.1 %all-to-all-start.2 = ((f32[4,1,16,16,256]{4,3,2,1,0:T(8,128)}), f32[4,1,16,16,256]{4,3,2,1,0:T(8,128)}, u32[]{:S(2)}, u32[]{:S(2)}) async-start(f32[4,1,16,16,256]{4,3,2,1,0:T(8,128)} %copy.23), calls=%async_computation.2 | async-start | bytes 2097152 | tf_op jit(solution)/shard_map/all_to_all | solution.py:30
  132.6 10.4 %copy-start.3 = (f32[32]{0:T(128)S(1)}, f32[32]{0:T(128)}, u32[]{:S(2)}) copy-start(f32[32]{0:T(128)} %param.13) | copy-start | bytes 388
  134.1 6.4 %collective-permute-start = (f32[32,16,1]{2,1,0:T(8,128)S(1)}, f32[32,16,1]{2,1,0:T(8,128)S(1)}, u32[]{:S(2)}, u32[]{:S(2)}) collective-permute-start(f32[32,16,1]{2,1,0:T(8,128)S(1)} %get-tuple-element.12), channel_id=1, source_target_pairs={{0,64},{64,128},{128,192},{192,0},{1,65},{65,129},{129,193},{193,1... | collective-permute-start | bytes 6152 | tf_op jit(solution)/shard_map/ppermute | solution.py:42
  134.2 6.4 %collective-permute-start.1 = (f32[32,16,1]{2,1,0:T(8,128)S(1)}, f32[32,16,1]{2,1,0:T(8,128)S(1)}, u32[]{:S(2)}, u32[]{:S(2)}) collective-permute-start(f32[32,16,1]{2,1,0:T(8,128)S(1)} %get-tuple-element.11), channel_id=1, source_target_pairs={{64,0},{128,64},{192,128},{0,192},{65,1},{129,65},{193,129},{1,193... | collective-permute-start | bytes 6152 | tf_op jit(solution)/shard_map/ppermute | solution.py:43
  136.2 4.4 %collective-permute-start.2 = (f32[32,1,256]{2,1,0:T(1,128)S(1)}, f32[32,1,256]{2,1,0:T(1,128)S(1)}, u32[]{:S(2)}, u32[]{:S(2)}) collective-permute-start(f32[32,1,256]{2,1,0:T(1,128)S(1)} %get-tuple-element.9), channel_id=1, source_target_pairs={{1,0},{2,1},{3,2},{4,3},{5,4},{6,5},{7,6},{8,7},{9,8},{10,9},{11,1... | collective-permute-start | bytes 98312 | tf_op jit(solution)/shard_map/ppermute | solution.py:43
  136.3 6.7 %collective-permute-start.3 = (f32[32,1,256]{2,1,0:T(1,128)S(1)}, f32[32,1,256]{2,1,0:T(1,128)S(1)}, u32[]{:S(2)}, u32[]{:S(2)}) collective-permute-start(f32[32,1,256]{2,1,0:T(1,128)S(1)} %get-tuple-element.10), channel_id=1, source_target_pairs={{0,1},{1,2},{2,3},{3,4},{4,5},{5,6},{6,7},{7,8},{8,9},{9,10},{10,1... | collective-permute-start | bytes 98312 | tf_op jit(solution)/shard_map/ppermute | solution.py:42
where the time goes:
time: 147 us; the launch traced here: 145 us
  waiting for transfers between devices  57 us (39%)
  local copies, waits for them, and re-layouts  34.9 us (24%)
  starting transfers between devices  25.5 us (17%)
  matrix products  19.4 us (13%)
  between operations  4.18 us (3%)
  other arithmetic  3.57 us (2%)
    all_to_all x1, waiting for transfers between devices, per_device(): lax.all_to_all(outgoing, 'tile', split_axis=0, concat_axis=0, tiled=True)  26.7 us
    all_to_all x2, waiting for transfers between devices, several_exchanges(): lax.all_to_all(piece, axis, split_axis=0, concat_axis=0, tiled=True)  24.3 us
    all_to_all x3, local copies, waits for them, and re-layouts, per_device(): lax.all_to_all(outgoing, 'tile', split_axis=0, concat_axis=0, tiled=True)  12.7 us
    all_to_all x1, starting transfers between devices, per_device(): lax.all_to_all(outgoing, 'tile', split_axis=0, concat_axis=0, tiled=True)  12.1 us
    dot_general x1, matrix products, per_device(): jnp.einsum('fpc,cx->xfp', thinned, col_weights, precision=lax.Precision.H...  11.2 us
    all_to_all x2, starting transfers between devices, several_exchanges(): lax.all_to_all(piece, axis, split_axis=0, concat_axis=0, tiled=True)  10.8 us
    dot_general x1, matrix products, per_device(): jnp.einsum('pr,frc->fpc', row_weights, child_block, precision=lax.Precisi...  8.12 us
    dynamic_update_slice x1, local copies, waits for them, and re-layouts, per_device(): lax.dynamic_update_slice(framed, column_slab, (jnp.int32(0), jnp.int32(0)...  6.74 us
  transfers between devices with their start and end apart: 7, of which 6 were waited for; matrix products, arithmetic and copies ran while one was open for 1% of the time, Pallas kernels for 0%

commit v1 on v0

v1 whole, which is shorter than its diff:
```python
import jax
import jax.numpy as jnp
from jax import lax
from jax.experimental import pallas as pl
from jax.experimental.pallas import tpu as pltpu
from jax.sharding import PartitionSpec as P

MESH = pl.DeviceIdType.MESH
CELL = 8
FC = 16
XB = 16
LANES = XB * FC
TILED = LANES // 128


def swap_rows_and_groups(v):
    sub = lax.broadcasted_iota(jnp.int32, v.shape, 0)
    lane = lax.broadcasted_iota(jnp.int32, v.shape, 1)
    for d in (1, 2, 4):
        w = FC * d
        low = pltpu.roll(pltpu.roll(v, CELL - d, 0), w, 1)
        high = pltpu.roll(pltpu.roll(v, d, 0), 128 - w, 1)
        sbit, lbit = (sub & d) != 0, (lane & w) != 0
        v = jnp.where(sbit == lbit, v, jnp.where(lbit, low, high))
    return v


def exchange_kernel(
    offs, rate, g_ref, prio_ref, par_ref, out_ref,
    gt, snd, slab, half, q, mrg, nat, part, prit, edge, halo, fin, parv, outv,
    ps, os, zs, zr, ys, yr, hs, hr,
):
    n, me = lax.axis_index("nest"), lax.axis_index("tile")
    tiles, nests = lax.axis_size("tile"), lax.axis_size("nest")
    cols, rows = tiles * XB, tiles * CELL
    own = par_ref.shape[1]
    chunks = snd.shape[0]
    top, left = offs[n, 0], offs[n, 1]

    span = min(128, own)
    taken = [
        pltpu.make_async_copy(par_ref.at[:, pl.ds(b * span, span)], parv.at[b], ps.at[b]) for b in range(own // span)
    ]
    for c in taken:
        c.start()

    barrier = pltpu.get_barrier_semaphore()

    @pl.loop(1, tiles)
    def _(j):
        pl.semaphore_signal(barrier, inc=1, device_id=(n, lax.rem(me + j, tiles)), device_id_type=MESH)

    for dn in range(1, nests):
        pl.semaphore_signal(barrier, inc=1, device_id=(lax.rem(n + dn, nests), me), device_id_type=MESH)

    def prepare(k):
        wide = min(128, cols)
        for b in range(cols // wide):
            gt[k, b * wide : (b + 1) * wide, :] = g_ref[k * 128 : (k + 1) * 128, b * wide : (b + 1) * wide].T
        gt[k, cols : cols + 8, :] = gt[k, 0:8, :]

        @pl.loop(0, tiles, step=4)
        def _(j0):
            for dj in range(4):
                for h in range(2):
                    s = lax.rem(XB * (j0 + dj) + 8 * h - left + cols, cols)
                    snd[k, j0 + dj, h] = swap_rows_and_groups(gt[k, pl.ds(s, 8), :])

    def send_tiles(k):
        @pl.loop(0, tiles - 1)
        def _(i):
            j = lax.select(lax.rem(i, 2) == 0, i // 2 + 1, tiles - 1 - i // 2)
            d = lax.rem(me + j, tiles)
            pltpu.make_async_remote_copy(
                src_ref=snd.at[k, d],
                dst_ref=slab[k].at[:, pl.ds(pl.multiple_of(CELL * me, CELL), CELL), :],
                send_sem=zs.at[k],
                recv_sem=zr.at[k],
                device_id=(n, d),
                device_id_type=MESH,
            ).start()

        slab[k][:, pl.ds(pl.multiple_of(CELL * me, CELL), CELL), :] = snd[k, me]

    def send_nests(k):
        got = slab[k].at[:, pl.ds(0, rows - CELL), :]
        pltpu.make_async_copy(got, got, zr.at[k]).wait()
        slab[k][:, rows : rows + 8, :] = slab[k][:, 0:8, :]

        @pl.loop(0, rows // 8)
        def _(g):
            s = lax.rem(8 * g - top + rows, rows)
            for t in range(TILED):
                half[k, t, pl.ds(pl.multiple_of(8 * g, 8), 8), :] = slab[k][t, pl.ds(s, 8), :]

        for dn in range(1, nests):
            b = lax.rem(n + dn, nests)
            start = pl.multiple_of(lax.rem(b * own, rows), own)
            pltpu.make_async_remote_copy(
                src_ref=half.at[k, :, pl.ds(start, own), :],
                dst_ref=q.at[k, n],
                send_sem=ys.at[k],
                recv_sem=yr.at[k],
                device_id=(b, me),
                device_id_type=MESH,
            ).start()
        mine = pl.multiple_of(lax.rem(n * own, rows), own)

        @pl.loop(0, own // 8)
        def _(g):
            r = pl.multiple_of(8 * g, 8)
            q[k, n, :, pl.ds(r, 8), :] = half[k, :, pl.ds(mine + r, 8), :]

    def to_rows(dst):
        for lb in range(TILED):
            for yb in range(own // span):
                dst[lb, yb * span : (yb + 1) * span, :] = nat[
                    lb * 128 : (lb + 1) * 128, yb * span : (yb + 1) * span
                ].T

    def own_rows():
        for x in range(XB):
            nat[x * FC : (x + 1) * FC, :] = jnp.broadcast_to(prio_ref[x : x + 1, :].astype(jnp.float32), (FC, own))
        to_rows(prit)
        for c in taken:
            c.wait()
        for k in range(chunks):
            for x in range(XB):
                for b in range(own // span):
                    nat[x * FC : (x + 1) * FC, b * span : (b + 1) * span] = parv[b, pl.ds(k * LANES + x, FC, stride=XB), :]
            to_rows(part.at[k])

    packs = min(8, own // 8)
    packed = own // packs
    lane = lax.broadcasted_iota(jnp.int32, (8, 128), 1)

    def merge(k):
        got = q.at[k, pl.ds(0, nests - 1)]
        pltpu.make_async_copy(got, got, yr.at[k]).wait()

        @pl.loop(0, own // 8)
        def _(g):
            r = pl.ds(pl.multiple_of(8 * g, 8), 8)
            v, p = part[k, :, r, :], prit[:, r, :]
            for m in range(nests):
                v = jnp.where(p == float(m), q[k, m, :, r, :], v)
            mrg[k, :, pl.ds(pl.multiple_of(8 * g + 8, 8), 8), :] = v

        for i in range(packed // 8):
            first = last = jnp.zeros((8, 128), jnp.float32)
            for j in range(packs):
                r = 8 + packed * j + 8 * i
                a, b = mrg[k, 0, r : r + 8, :], mrg[k, TILED - 1, r : r + 8, :]
                here = lane // FC == j
                first = jnp.where(here, pltpu.roll(a, FC * j, 1) if j else a, first)
                shift = (FC * j + FC) % 128
                last = jnp.where(here, pltpu.roll(b, shift, 1) if shift else b, last)
            edge[k, 0, 8 * i : 8 * i + 8, :] = first
            edge[k, 1, 8 * i : 8 * i + 8, :] = last

        east, west = lax.rem(me + 1, tiles), lax.rem(me + tiles - 1, tiles)
        up, down = lax.rem(n + 1, nests), lax.rem(n + nests - 1, nests)
        moves = (
            (edge.at[k, 0], halo.at[k, 0], (n, west)),
            (edge.at[k, 1], halo.at[k, 1], (n, east)),
            (mrg.at[k, :, pl.ds(8, 8), :], mrg.at[k, :, pl.ds(own + 8, 8), :], (down, me)),
            (mrg.at[k, :, pl.ds(own, 8), :], mrg.at[k, :, pl.ds(0, 8), :], (up, me)),
        )
        copies = [
            pltpu.make_async_remote_copy(
                src_ref=s, dst_ref=d, send_sem=hs.at[k, i], recv_sem=hr.at[k, i], device_id=to, device_id_type=MESH
            )
            for i, (s, d, to) in enumerate(moves)
        ]
        for c in copies:
            c.start()
        return copies

    def finish(k, copies):
        for c in copies:
            c.wait()
        mrg[k, :, 7:8, :] = jnp.where(n == 0, mrg[k, :, 8:9, :], mrg[k, :, 7:8, :])
        mrg[k, :, own + 8 : own + 9, :] = jnp.where(
            n == nests - 1, mrg[k, :, own + 7 : own + 8, :], mrg[k, :, own + 8 : own + 9, :]
        )
        r = jnp.zeros((8, 128), jnp.float32)
        for f in range(FC):
            r = jnp.where(lax.rem(lane, FC) == f, rate[k * FC + f], r)

        for j in range(packs):
            @pl.loop(0, packed // 8)
            def _(i):
                o = pl.multiple_of(packed * j + 8 * i, 8)
                e = halo[k, 0, pl.ds(pl.multiple_of(8 * i, 8), 8), :]
                w = halo[k, 1, pl.ds(pl.multiple_of(8 * i, 8), 8), :]
                es, ws = (128 - FC - FC * j) % 128, (128 - FC * j) % 128
                e = pltpu.roll(e, es, 1) if es else e
                w = pltpu.roll(w, ws, 1) if ws else w
                mid = [mrg[k, t, pl.ds(o + 8, 8), :] for t in range(TILED)]
                east = [pltpu.roll(c, 128 - FC, 1) for c in mid] + [e]
                west = [w] + [pltpu.roll(c, FC, 1) for c in mid]
                for t in range(TILED):
                    c = mid[t]
                    north, south = mrg[k, t, pl.ds(o + 9, 8), :], mrg[k, t, pl.ds(o + 7, 8), :]
                    east_side = jnp.where(lane >= 128 - FC, east[t + 1], east[t])
                    west_side = jnp.where(lane < FC, west[t], west[t + 1])
                    fin[t, pl.ds(o, 8), :] = c + r * (east_side + west_side + north + south - 4.0 * c)

        for lb in range(TILED):
            for yb in range(own // span):
                t = fin[lb, yb * span : (yb + 1) * span, :].T
                for x in range(8):
                    outv[yb, pl.ds(k * LANES + lb * 8 + x, FC, stride=XB), :] = t[x * FC : (x + 1) * FC, :]
        r = pl.ds(k * LANES, LANES)
        for b in range(own // span):
            c = pltpu.make_async_copy(outv.at[b, r, :], out_ref.at[r, pl.ds(b * span, span)], os.at[k, b])
            c.start()
            given.append(c)

    prepare(0)
    pl.semaphore_wait(barrier, tiles - 1 + nests - 1)
    send_tiles(0)
    for k in range(1, chunks):
        prepare(k)
        send_tiles(k)
    own_rows()
    flights, given = [], []
    for k in range(chunks):
        send_nests(k)
        if k:
            flights.append(merge(k - 1))
            if k > 1:
                finish(k - 2, flights[k - 2])
    flights.append(merge(chunks - 1))
    if chunks > 1:
        finish(chunks - 2, flights[chunks - 2])
    finish(chunks - 1, flights[chunks - 1])
    for c in given:
        c.wait()
    for k in range(chunks):
        sent = slab[k].at[:, pl.ds(0, rows - CELL), :]
        pltpu.make_async_copy(sent, sent, zs.at[k]).wait()
        sent = q.at[k, pl.ds(0, nests - 1)]
        pltpu.make_async_copy(sent, sent, ys.at[k]).wait()


def exchange(offs, rate, g, prio, par, tiles, nests):
    own = par.shape[1]
    fields = par.shape[0] // XB
    chunks = fields // FC
    cols, rows = tiles * XB, tiles * CELL
    span = min(128, own)
    f32 = jnp.float32
    vm = pl.BlockSpec(memory_space=pltpu.VMEM)
    sm = pl.BlockSpec(memory_space=pltpu.SMEM)
    dma = pltpu.SemaphoreType.DMA
    return pl.pallas_call(
        exchange_kernel,
        out_shape=jax.ShapeDtypeStruct(par.shape, f32),
        in_specs=[sm, sm, vm, vm, pl.BlockSpec(memory_space=pl.ANY)],
        out_specs=pl.BlockSpec(memory_space=pl.ANY),
        scratch_shapes=[
            pltpu.VMEM((chunks, cols + 8, 128), f32),
            pltpu.VMEM((chunks, tiles, TILED, CELL, 128), f32),
            [pltpu.VMEM((TILED, rows + 8, 128), f32) for _ in range(chunks)],
            pltpu.VMEM((chunks, TILED, rows, 128), f32),
            pltpu.VMEM((chunks, nests, TILED, own, 128), f32),
            pltpu.VMEM((chunks, TILED, own + 16, 128), f32),
            pltpu.VMEM((LANES, own), f32),
            pltpu.VMEM((chunks, TILED, own, 128), f32),
            pltpu.VMEM((TILED, own, 128), f32),
            pltpu.VMEM((chunks, 2, own // min(8, own // 8), 128), f32),
            pltpu.VMEM((chunks, 2, own // min(8, own // 8), 128), f32),
            pltpu.VMEM((TILED, own, 128), f32),
            pltpu.VMEM((own // span, *par.shape[:1], span), f32),
            pltpu.VMEM((own // span, *par.shape[:1], span), f32),
            dma((own // span,)), dma((chunks, own // span)),
            dma((chunks,)), dma((chunks,)), dma((chunks,)), dma((chunks,)), dma((chunks, 4)), dma((chunks, 4)),
        ],
        compiler_params=pltpu.CompilerParams(
            collective_id=0, has_side_effects=True, vmem_limit_bytes=40 * 1024 * 1024
        ),
    )(offs, rate, g, prio, par)


def per_device(child_fields, row_weights, col_weights, nest_offsets, priority, parent_old, smooth_rate):
    fields, strip, own = parent_old.shape
    tiles, nests = lax.axis_size("tile"), lax.axis_size("nest")
    child = child_fields[0].reshape(fields // FC, FC, *child_fields.shape[2:])
    high = lax.Precision.HIGH
    thinned = jnp.einsum("pr,kfrc->kpfc", row_weights, child, precision=high)
    thinned = thinned.reshape(fields * CELL, -1)
    g = jnp.einsum("mc,cx->mx", thinned, col_weights, precision=high)
    out = exchange(nest_offsets, smooth_rate, g, priority, parent_old.reshape(fields * strip, own), tiles, nests)
    return out.reshape(fields, strip, own)


def solution(mesh):
    return jax.shard_map(
        per_device,
        mesh=mesh,
        in_specs=(
            P("nest", None, "tile", None),
            P(),
            P(),
            P(),
            P("tile", "nest"),
            P(None, "tile", "nest"),
            P(),
        ),
        out_specs=P(None, "tile", "nest"),
        check_vma=False,
    )
```

time: 147 us -> 74.9 us (0.51)
  the two profiles are of different devices: /device:TPU:8 before, /device:TPU:1 now
where the time goes in v1:
time: 74.9 us; the launch traced here: 74.8 us
  Pallas kernels  59.9 us (80%)
  matrix products  11.3 us (15%)
  local copies, waits for them, and re-layouts  3.5 us (5%)
    pallas_call x1, Pallas kernels, exchange(): pl.pallas_call(exchange_kernel, out_shape=jax.ShapeDtypeStruct(par.shape,...  59.9 us
    dot_general x1, matrix products, per_device(): g = jnp.einsum('mc,cx->mx', thinned, col_weights, precision=high)  5.93 us
    dot_general x1, matrix products, per_device(): thinned = jnp.einsum('pr,kfrc->kpfc', row_weights, child, precision=high)  5.38 us
    transpose x1, local copies, waits for them, and re-layouts, per_device(): thinned = jnp.einsum('pr,kfrc->kpfc', row_weights, child, precision=high)  1.82 us
    unnamed x14, local copies, waits for them, and re-layouts  1.67 us

profile of v1, /device:TPU:1, one launch (start us, length us, event | category | flops | bytes accessed | tf_op | source)
XLA Modules:
  0.0 74.8 jit_solution(10806806194309237339)
XLA Ops:
  0.0 0.0 copy-start
  0.0 0.7 copy-done
  0.7 0.0 copy-start.4
  0.7 5.4 %convolution_bitcast_fusion = f32[2,8,16,3072]{3,1,2,0:T(8,128)S(1)} fusion(f32[2,16,24,3072]{3,2,1,0:T(8,128)} %bitcast.17, f32[8,24]{1,0:T(8,128)S(1)} %copy-done), kind=kOutput, calls=%fused_computation | convolution fusion | flops 113246208 | bytes 12583680 | tf_op jit(solution)/shard_map/pr,kfrc->kpfc/dot_general | solution.py:291
  6.1 1.8 %copy.9 = f32[2,8,16,3072]{3,2,1,0:T(8,128)S(1)} copy(f32[2,8,16,3072]{3,1,2,0:T(8,128)S(1)} %convolution_bitcast_fusion) | data formatting | bytes 6291456 | tf_op jit(solution)/shard_map/pr,kfrc->kpfc/transpose | solution.py:291
  7.9 0.0 copy-start.5
  7.9 0.0 copy-start.1
  7.9 0.0 copy-start.2
  7.9 0.0 copy-start.3
  8.0 0.1 copy-done.4
  8.0 5.9 %fusion.1.g_ref = f32[256,1024]{1,0:T(8,128)S(1)} fusion(f32[256,3072]{1,0:T(8,128)S(1)} %bitcast.16, f32[3072,1024]{1,0:T(8,128)S(1)} %copy-done.4), kind=kOutput, calls=%fused_computation.2 | convolution fusion | flops 4831838208 | bytes 16777216 | tf_op jit(solution)/shard_map/mc,cx->mx/dot_general | solution.py:293
  14.0 0.0 copy-done.5
  14.0 0.1 copy.10.offs
  14.1 0.0 copy-done.1
  14.1 0.0 copy-done.2
  14.1 0.0 copy-done.3
  14.1 59.9 %shard_map.73 = f32[512,256]{1,0:T(8,128)S(1)} custom-call(s32[4,2]{1,0:T(4,128)S(1)} %copy.10.offs, f32[32]{0:T(128)S(1)} %copy-done.3, f32[256,1024]{1,0:T(8,128)S(1)} %fusion.1.g_ref, s32[16,256]{1,0:T(8,128)S(1)} %copy-done.2, f32[512,256]{1,0:T(8,128)S(1)} %bitcast.15), custom_call_target="tpu_custom_call" | custom-call | tf_op jit(solution)/shard_map/pallas_call | solution.py:257
  74.0 0.8 %copy.13 = f32[32,16,256]{2,1,0:T(8,128)} copy(f32[32,16,256]{2,1,0:T(8,128)S(1)} %bitcast.14) | data formatting | bytes 1048576
Async XLA Ops:
  0.0 0.7 copy-start
  0.7 7.3 %copy-start.4 = (f32[3072,1024]{1,0:T(8,128)S(1)}, f32[3072,1024]{1,0:T(8,128)}, u32[]{:S(2)}) copy-start(f32[3072,1024]{1,0:T(8,128)} %param.9) | copy-start | bytes 37748740
  7.9 6.1 %copy-start.5 = (s32[4,2]{0,1:T(2,128)S(1)}, s32[4,2]{0,1:T(2,128)}, u32[]{:S(2)}) copy-start(s32[4,2]{0,1:T(2,128)} %param.10) | copy-start | bytes 100
  7.9 6.1 %copy-start.1 = (f32[32,16,256]{2,1,0:T(8,128)S(1)}, f32[32,16,256]{2,1,0:T(8,128)}, u32[]{:S(2)}) copy-start(f32[32,16,256]{2,1,0:T(8,128)} %param.12) | copy-start | bytes 1572868
  7.9 6.1 %copy-start.2 = (s32[16,256]{1,0:T(8,128)S(1)}, s32[16,256]{1,0:T(8,128)}, u32[]{:S(2)}) copy-start(s32[16,256]{1,0:T(8,128)} %prio_ref.1) | copy-start | bytes 49156
  7.9 6.1 %copy-start.3 = (f32[32]{0:T(128)S(1)}, f32[32]{0:T(128)}, u32[]{:S(2)}) copy-start(f32[32]{0:T(128)} %rate.1) | copy-start | bytes 388

commit v2 on v1

v2 whole, which is shorter than its diff:
```python
import jax
import jax.numpy as jnp
from jax import lax
from jax.experimental import pallas as pl
from jax.experimental.pallas import tpu as pltpu
from jax.sharding import PartitionSpec as P

MESH = pl.DeviceIdType.MESH
CELL = 8
FC = 16
XB = 16
TILED = XB * FC // 128
AHEAD = 3
f32, bf16 = jnp.float32, jnp.bfloat16


def swap_rows_and_groups(v):
    sub = lax.broadcasted_iota(jnp.int32, v.shape, 0)
    lane = lax.broadcasted_iota(jnp.int32, v.shape, 1)
    for d in (1, 2, 4):
        w = FC * d
        low = pltpu.roll(pltpu.roll(v, CELL - d, 0), w, 1)
        high = pltpu.roll(pltpu.roll(v, d, 0), 128 - w, 1)
        sbit, lbit = (sub & d) != 0, (lane & w) != 0
        v = jnp.where(sbit == lbit, v, jnp.where(lbit, low, high))
    return v


def two_parts(v):
    high = v.astype(bf16)
    return high, (v - high.astype(f32)).astype(bf16)


def mm(a, b):
    return jnp.dot(a, b, preferred_element_type=f32)


def kernel(
    offs, rate, child, row_w, col_w, prio_ref, par_ref, out_ref,
    xbuf, cbuf, whi, wlo, wide_w, acc,
    gt, snd, slab, half, q, mrg, nat, part, prit, edge, halo, fin, parv, outv,
    cs, ws, ps, os, zs, zr, ys, yr, hs, hr,
):
    n, me = lax.axis_index("nest"), lax.axis_index("tile")
    tiles, nests = lax.axis_size("tile"), lax.axis_size("nest")
    cols, rows = tiles * XB, tiles * CELL
    own = par_ref.shape[1]
    chunks, pieces, depth, piece = xbuf.shape
    crow = row_w.shape[1]
    top, left = offs[n, 0], offs[n, 1]
    high = FC * CELL

    def child_copy(k, c):
        start = c * piece if isinstance(c, int) else pl.multiple_of(c * piece, 128)
        return pltpu.make_async_copy(
            child.at[pl.ds(k * depth, depth), pl.ds(start, piece)], xbuf.at[k, c], cs.at[k, c]
        )

    def weight_copy(c):
        start = c * piece if isinstance(c, int) else pl.multiple_of(c * piece, 128)
        return pltpu.make_async_copy(col_w.at[pl.ds(start, piece), :], cbuf.at[c], ws.at[c])

    for c in range(min(AHEAD, pieces)):
        child_copy(0, c).start()
        weight_copy(c).start()

    barrier = pltpu.get_barrier_semaphore()

    @pl.loop(1, tiles)
    def _(j):
        pl.semaphore_signal(barrier, inc=1, device_id=(n, lax.rem(me + j, tiles)), device_id_type=MESH)

    for dn in range(1, nests):
        pl.semaphore_signal(barrier, inc=1, device_id=(lax.rem(n + dn, nests), me), device_id_type=MESH)

    def spread_row_weights():
        a = lax.broadcasted_iota(jnp.int32, (high, CELL), 0)
        b = lax.broadcasted_iota(jnp.int32, (high, CELL), 1)
        down = (a // FC == b).astype(f32).astype(bf16)
        a = lax.broadcasted_iota(jnp.int32, (crow, depth), 0)
        b = lax.broadcasted_iota(jnp.int32, (crow, depth), 1)
        across = (lax.rem(b, crow) == a).astype(f32).astype(bf16)
        a = lax.broadcasted_iota(jnp.int32, (high, depth), 0)
        b = lax.broadcasted_iota(jnp.int32, (high, depth), 1)
        same = lax.rem(a, FC) == b // crow
        for i, w in enumerate(two_parts(row_w[...])):
            full = mm(mm(down, w).astype(bf16), across)
            wide_w[i * high : (i + 1) * high, :] = jnp.where(same, full, 0.0).astype(bf16)

    step = min(256, piece)
    block = min(256, cols)

    def compute(k):
        acc[k] = jnp.zeros(acc.shape[1:], f32)

        @pl.loop(0, pieces)
        def _(c):
            child_copy(k, c).wait()
            if k == 0:
                weight_copy(c).wait()

                @pl.when(c + AHEAD < pieces)
                def _():
                    child_copy(0, c + AHEAD).start()
                    weight_copy(c + AHEAD).start()

            if k + 1 < chunks:
                child_copy(k + 1, c).start()
            left_high, left_low = [], []
            for s in range(piece // step):
                xh, xl = two_parts(xbuf[k, c, :, s * step : (s + 1) * step])
                t = mm(wide_w[...], xh)
                t = t[:high] + t[high:] + mm(wide_w[0:high, :], xl)
                th, tl = two_parts(t)
                left_high.append(th)
                left_low.append(tl)
            a_high = jnp.concatenate(left_high, 1)
            a = jnp.concatenate([a_high, jnp.concatenate(left_low, 1)], 0)
            for b in range(cols // block):
                span = pl.ds(b * block, block)
                if k == 0:
                    wh, wl = two_parts(cbuf[c, :, span])
                    whi[c, :, span] = wh
                    wlo[c, :, span] = wl
                else:
                    wh, wl = whi[c, :, span], wlo[c, :, span]
                u = mm(a, wh)
                acc[k, :, span] += u[:high] + u[high:] + mm(a_high, wl)

    def turn(k):
        wide = min(128, cols)
        for b in range(cols // wide):
            gt[k, b * wide : (b + 1) * wide, :] = acc[k, :, b * wide : (b + 1) * wide].T
        gt[k, cols : cols + 8, :] = gt[k, 0:8, :]

    def send_tiles(k, h):
        @pl.loop(0, tiles, step=8)
        def _(j0):
            for dj in range(8):
                s = lax.rem(XB * (j0 + dj) + 8 * h - left + cols, cols)
                snd[k, h, j0 + dj] = swap_rows_and_groups(gt[k, pl.ds(s, 8), :])

        mine = pl.ds(pl.multiple_of(CELL * me, CELL), CELL)

        @pl.loop(0, tiles - 1)
        def _(i):
            j = lax.select(lax.rem(i, 2) == 0, i // 2 + 1, tiles - 1 - i // 2)
            d = lax.rem(me + j, tiles)
            pltpu.make_async_remote_copy(
                src_ref=snd.at[k, h, d],
                dst_ref=slab[k][h].at[mine, :],
                send_sem=zs.at[k, h],
                recv_sem=zr.at[k, h],
                device_id=(n, d),
                device_id_type=MESH,
            ).start()

        slab[k][h][mine, :] = snd[k, h, me]

    def send_nests(k, h):
        here = slab[k][h]
        got = here.at[pl.ds(0, rows - CELL), :]
        pltpu.make_async_copy(got, got, zr.at[k, h]).wait()
        here[rows : rows + 8, :] = here[0:8, :]

        @pl.loop(0, rows // 8, step=8)
        def _(g0):
            for dg in range(8):
                g = g0 + dg
                s = lax.rem(8 * g - top + rows, rows)
                half[k, h, pl.ds(pl.multiple_of(8 * g, 8), 8), :] = here[pl.ds(s, 8), :]

        for dn in (2, 1, 3):
            b = lax.rem(n + dn, nests)
            start = pl.multiple_of(lax.rem(b * own, rows), own)
            pltpu.make_async_remote_copy(
                src_ref=half.at[k, h, pl.ds(start, own), :],
                dst_ref=q.at[k, h, n],
                send_sem=ys.at[k, h],
                recv_sem=yr.at[k, h],
                device_id=(b, me),
                device_id_type=MESH,
            ).start()
        mine = pl.multiple_of(lax.rem(n * own, rows), own)

        @pl.loop(0, own // 8)
        def _(g):
            r = pl.multiple_of(8 * g, 8)
            q[k, h, n, pl.ds(r, 8), :] = half[k, h, pl.ds(mine + r, 8), :]

    span = min(128, own)
    taken = [
        pltpu.make_async_copy(par_ref.at[:, pl.ds(b * span, span)], parv.at[b], ps.at[b]) for b in range(own // span)
    ]

    def to_rows(dst):
        for lb in range(TILED):
            for yb in range(own // span):
                dst[lb, yb * span : (yb + 1) * span, :] = nat[
                    lb * 128 : (lb + 1) * 128, yb * span : (yb + 1) * span
                ].T

    def own_rows():
        for x in range(XB):
            nat[x * FC : (x + 1) * FC, :] = jnp.broadcast_to(prio_ref[x : x + 1, :].astype(f32), (FC, own))
        to_rows(prit)
        for c in taken:
            c.wait()
        for k in range(chunks):
            for x in range(XB):
                for b in range(own // span):
                    nat[x * FC : (x + 1) * FC, b * span : (b + 1) * span] = parv[
                        b, pl.ds(k * XB * FC + x, FC, stride=XB), :
                    ]
            to_rows(part.at[k])

    packs = min(8, own // 8)
    packed = own // packs
    lane = lax.broadcasted_iota(jnp.int32, (8, 128), 1)
    east, west = lax.rem(me + 1, tiles), lax.rem(me + tiles - 1, tiles)
    up, down = lax.rem(n + 1, nests), lax.rem(n + nests - 1, nests)
    flights, given = {}, []

    def merge(k, h):
        got = q.at[k, h, pl.ds(0, nests - 1)]
        pltpu.make_async_copy(got, got, yr.at[k, h]).wait()

        @pl.loop(0, own // 8, step=4)
        def _(g0):
            for dg in range(4):
                r = pl.ds(pl.multiple_of(8 * (g0 + dg), 8), 8)
                v, p = part[k, h, r, :], prit[h, r, :]
                for m in range(nests):
                    v = jnp.where(p == float(m), q[k, h, m, r, :], v)
                mrg[k, h, pl.ds(pl.multiple_of(8 * (g0 + dg) + 8, 8), 8), :] = v

        moves = [
            (mrg.at[k, h, pl.ds(8, 8), :], mrg.at[k, h, pl.ds(own + 8, 8), :], (down, me)),
            (mrg.at[k, h, pl.ds(own, 8), :], mrg.at[k, h, pl.ds(0, 8), :], (up, me)),
        ]
        for side, tile, to in ((0, 0, west), (1, TILED - 1, east)):
            if h != tile:
                continue
            for i in range(packed // 8):
                e = jnp.zeros((8, 128), f32)
                for j in range(packs):
                    a = mrg[k, h, 8 + packed * j + 8 * i : 16 + packed * j + 8 * i, :]
                    shift = (FC * (j + side)) % 128
                    e = jnp.where(lane // FC == j, pltpu.roll(a, shift, 1) if shift else a, e)
                edge[k, side, 8 * i : 8 * i + 8, :] = e
            moves.append((edge.at[k, side], halo.at[k, side], (n, to)))
        copies = [
            pltpu.make_async_remote_copy(
                src_ref=s, dst_ref=d, send_sem=hs.at[k, h, i], recv_sem=hr.at[k, h, i], device_id=to, device_id_type=MESH
            )
            for i, (s, d, to) in enumerate(moves)
        ]
        for c in copies:
            c.start()
        flights.setdefault(k, []).extend(copies)

    def finish(k):
        for c in flights[k]:
            c.wait()
        mrg[k, :, 7:8, :] = jnp.where(n == 0, mrg[k, :, 8:9, :], mrg[k, :, 7:8, :])
        mrg[k, :, own + 8 : own + 9, :] = jnp.where(
            n == nests - 1, mrg[k, :, own + 7 : own + 8, :], mrg[k, :, own + 8 : own + 9, :]
        )
        r = jnp.zeros((8, 128), f32)
        for f in range(FC):
            r = jnp.where(lax.rem(lane, FC) == f, rate[k * FC + f], r)

        for j in range(packs):
            @pl.loop(0, packed // 8)
            def _(i):
                o = pl.multiple_of(packed * j + 8 * i, 8)
                e = halo[k, 0, pl.ds(pl.multiple_of(8 * i, 8), 8), :]
                w = halo[k, 1, pl.ds(pl.multiple_of(8 * i, 8), 8), :]
                es, ws_ = (128 - FC - FC * j) % 128, (128 - FC * j) % 128
                e = pltpu.roll(e, es, 1) if es else e
                w = pltpu.roll(w, ws_, 1) if ws_ else w
                mid = [mrg[k, t, pl.ds(o + 8, 8), :] for t in range(TILED)]
                east_of = [pltpu.roll(c, 128 - FC, 1) for c in mid] + [e]
                west_of = [w] + [pltpu.roll(c, FC, 1) for c in mid]
                for t in range(TILED):
                    c = mid[t]
                    north, south = mrg[k, t, pl.ds(o + 9, 8), :], mrg[k, t, pl.ds(o + 7, 8), :]
                    east_side = jnp.where(lane >= 128 - FC, east_of[t + 1], east_of[t])
                    west_side = jnp.where(lane < FC, west_of[t], west_of[t + 1])
                    fin[t, pl.ds(o, 8), :] = c + r * (east_side + west_side + north + south - 4.0 * c)

        for lb in range(TILED):
            for yb in range(own // span):
                t = fin[lb, yb * span : (yb + 1) * span, :].T
                for x in range(8):
                    outv[yb, pl.ds(k * XB * FC + lb * 8 + x, FC, stride=XB), :] = t[x * FC : (x + 1) * FC, :]
        r = pl.ds(k * XB * FC, XB * FC)
        for b in range(own // span):
            c = pltpu.make_async_copy(outv.at[b, r, :], out_ref.at[r, pl.ds(b * span, span)], os.at[k, b])
            c.start()
            given.append(c)

    spread_row_weights()
    for k in range(chunks):
        compute(k)
        if k == 0:
            for c in taken:
                c.start()
            pl.semaphore_wait(barrier, tiles - 1 + nests - 1)
        turn(k)
        for h in range(TILED):
            send_tiles(k, h)
    own_rows()
    order = [(k, h) for k in range(chunks) for h in range(TILED)]
    for i, (k, h) in enumerate(order):
        send_nests(k, h)
        if i >= 2:
            merge(*order[i - 2])
            if order[i - 2][1] == TILED - 1 and i < len(order) - 1:
                finish(order[i - 2][0])
    for k, h in order[-2:]:
        if h == 0 and k > 0:
            finish(k - 1)
        merge(k, h)
    finish(chunks - 1)
    for c in given:
        c.wait()
    for k, h in order:
        sent = slab[k][h].at[pl.ds(0, rows - CELL), :]
        pltpu.make_async_copy(sent, sent, zs.at[k, h]).wait()
        sent = q.at[k, h, pl.ds(0, nests - 1)]
        pltpu.make_async_copy(sent, sent, ys.at[k, h]).wait()


def feedback(offs, rate, child, row_w, col_w, prio, par, tiles, nests):
    own = par.shape[1]
    chunks = par.shape[0] // XB // FC
    cols, rows = tiles * XB, tiles * CELL
    span = min(128, own)
    depth = FC * row_w.shape[1]
    width = child.shape[1]
    pieces = min(6, width // 128)
    piece = width // pieces
    packed = own // min(8, own // 8)
    vm = pl.BlockSpec(memory_space=pltpu.VMEM)
    sm = pl.BlockSpec(memory_space=pltpu.SMEM)
    hbm = pl.BlockSpec(memory_space=pl.ANY)
    dma = pltpu.SemaphoreType.DMA
    return pl.pallas_call(
        kernel,
        out_shape=jax.ShapeDtypeStruct(par.shape, f32),
        in_specs=[sm, sm, hbm, vm, hbm, vm, hbm],
        out_specs=hbm,
        scratch_shapes=[
            pltpu.VMEM((chunks, pieces, depth, piece), f32),
            pltpu.VMEM((pieces, piece, cols), f32),
            pltpu.VMEM((pieces, piece, cols), bf16),
            pltpu.VMEM((pieces, piece, cols), bf16),
            pltpu.VMEM((2 * FC * CELL, depth), bf16),
            pltpu.VMEM((chunks, FC * CELL, cols), f32),
            pltpu.VMEM((chunks, cols + 8, 128), f32),
            pltpu.VMEM((chunks, TILED, tiles, CELL, 128), f32),
            [[pltpu.VMEM((rows + 8, 128), f32) for _ in range(TILED)] for _ in range(chunks)],
            pltpu.VMEM((chunks, TILED, rows, 128), f32),
            pltpu.VMEM((chunks, TILED, nests, own, 128), f32),
            pltpu.VMEM((chunks, TILED, own + 16, 128), f32),
            pltpu.VMEM((XB * FC, own), f32),
            pltpu.VMEM((chunks, TILED, own, 128), f32),
            pltpu.VMEM((TILED, own, 128), f32),
            pltpu.VMEM((chunks, 2, packed, 128), f32),
            pltpu.VMEM((chunks, 2, packed, 128), f32),
            pltpu.VMEM((TILED, own, 128), f32),
            pltpu.VMEM((own // span, par.shape[0], span), f32),
            pltpu.VMEM((own // span, par.shape[0], span), f32),
            dma((chunks, pieces)), dma((pieces,)), dma((own // span,)), dma((chunks, own // span)),
            dma((chunks, TILED)), dma((chunks, TILED)), dma((chunks, TILED)), dma((chunks, TILED)),
            dma((chunks, TILED, 4)), dma((chunks, TILED, 4)),
        ],
        compiler_params=pltpu.CompilerParams(
            collective_id=0, has_side_effects=True, vmem_limit_bytes=60 * 1024 * 1024
        ),
    )(offs, rate, child, row_w, col_w, prio, par)


def per_device(child_fields, row_weights, col_weights, nest_offsets, priority, parent_old, smooth_rate):
    fields, strip, own = parent_old.shape
    tiles, nests = lax.axis_size("tile"), lax.axis_size("nest")
    child = child_fields.reshape(-1, child_fields.shape[3])
    par = parent_old.reshape(fields * strip, own)
    out = feedback(nest_offsets, smooth_rate, child, row_weights, col_weights, priority, par, tiles, nests)
    return out.reshape(fields, strip, own)


def solution(mesh):
    return jax.shard_map(
        per_device,
        mesh=mesh,
        in_specs=(
            P("nest", None, "tile", None),
            P(),
            P(),
            P(),
            P("tile", "nest"),
            P(None, "tile", "nest"),
            P(),
        ),
        out_specs=P(None, "tile", "nest"),
        check_vma=False,
    )
```

time: 74.9 us -> 71.5 us (0.955)
  the two profiles are of different devices: /device:TPU:1 before, /device:TPU:8 now
where the time goes in v2:
time: 71.5 us; the launch traced here: 71 us
  Pallas kernels  67.8 us (95%)
  local copies, waits for them, and re-layouts  3.2 us (4%)
    pallas_call x1, Pallas kernels, feedback(): pl.pallas_call(kernel, out_shape=jax.ShapeDtypeStruct(par.shape, f32), in...  67.8 us
    unnamed x2, local copies, waits for them, and re-layouts  3.2 us

profile of v2, /device:TPU:8, one launch (start us, length us, event | category | flops | bytes accessed | tf_op | source)
XLA Modules:
  0.0 71.0 jit_solution(14923332560892709773)
XLA Ops:
  0.0 1.3 %copy.8.offs = s32[4,2]{1,0:T(4,128)} copy(s32[4,2]{0,1:T(2,128)} %param.10) | data formatting | bytes 64 | tf_op args[3]
  1.3 67.8 %shard_map.73 = f32[512,256]{1,0:T(8,128)} custom-call(s32[4,2]{1,0:T(4,128)} %copy.8.offs, f32[32]{0:T(128)} %rate.1, f32[768,3072]{1,0:T(8,128)} %bitcast.3, f32[8,24]{1,0:T(8,128)} %row_w.1, f32[3072,1024]{1,0:T(8,128)} %col_w.1, s32[16,256]{1,0:T(8,128)} %prio_ref.1, f32[512,256]{1,0:T(8,128)} %bitcast.5), custom_call_target="tpu_custom_call" | custom-call | tf_op jit(solution)/shard_map/pallas_call | solution.py:349
  69.2 1.9 %copy.10 = f32[32,16,256]{2,1,0:T(8,128)} copy(f32[32,16,256]{2,1,0:T(8,128)} %bitcast.4) | data formatting | bytes 1048576

commit v3 on v2

--- a/solution.py
+++ b/solution.py
@@ -36,10 +36,10 @@
 
 
 def kernel(
-    offs, rate, child, row_w, col_w, prio_ref, par_ref, out_ref,
-    xbuf, cbuf, whi, wlo, wide_w, acc,
-    gt, snd, slab, half, q, mrg, nat, part, prit, edge, halo, fin, parv, outv,
-    cs, ws, ps, os, zs, zr, ys, yr, hs, hr,
+    offs_in, rate_in, child, row_in, col_w, prio_in, par_ref, out_ref,
+    offs, rate, row_w, prio_ref, xbuf, cbuf, whi, wlo, wide_w, acc,
+    gt, snd, land, relay, slab, half, q, mrg, nat, part, prit, edge, halo, fin, parv, outv,
+    ms, cs, ws, ps, os, zs, zr, fs, fr, ys, yr, hs, hr,
 ):
     n, me = lax.axis_index("nest"), lax.axis_index("tile")
     tiles, nests = lax.axis_size("tile"), lax.axis_size("nest")
@@ -47,7 +47,8 @@
     own = par_ref.shape[1]
     chunks, pieces, depth, piece = xbuf.shape
     crow = row_w.shape[1]
-    top, left = offs[n, 0], offs[n, 1]
+    chips, chip, core = tiles // 2, me // 2, lax.rem(me, 2)
+    other = 2 * chip + 1 - core
     high = FC * CELL
 
     def child_copy(k, c):
@@ -60,18 +61,29 @@
         start = c * piece if isinstance(c, int) else pl.multiple_of(c * piece, 128)
         return pltpu.make_async_copy(col_w.at[pl.ds(start, piece), :], cbuf.at[c], ws.at[c])
 
+    small = [
+        pltpu.make_async_copy(a, b, ms.at[i])
+        for i, (a, b) in enumerate(((row_in, row_w), (offs_in, offs), (rate_in, rate), (prio_in, prio_ref)))
+    ]
+    small[0].start()
     for c in range(min(AHEAD, pieces)):
         child_copy(0, c).start()
         weight_copy(c).start()
+    for c in small[1:]:
+        c.start()
 
     barrier = pltpu.get_barrier_semaphore()
-
-    @pl.loop(1, tiles)
+    peers = chips - 1 + nests - 1 + 2
+
+    @pl.loop(1, chips)
     def _(j):
-        pl.semaphore_signal(barrier, inc=1, device_id=(n, lax.rem(me + j, tiles)), device_id_type=MESH)
+        d = 2 * lax.rem(chip + j, chips) + core
+        pl.semaphore_signal(barrier, inc=1, device_id=(n, d), device_id_type=MESH)
 
     for dn in range(1, nests):
         pl.semaphore_signal(barrier, inc=1, device_id=(lax.rem(n + dn, nests), me), device_id_type=MESH)
+    for dt in (1, tiles - 1):
+        pl.semaphore_signal(barrier, inc=1, device_id=(n, lax.rem(me + dt, tiles)), device_id_type=MESH)
 
     def spread_row_weights():
         a = lax.broadcasted_iota(jnp.int32, (high, CELL), 0)
@@ -134,41 +146,63 @@
         gt[k, cols : cols + 8, :] = gt[k, 0:8, :]
 
     def send_tiles(k, h):
-        @pl.loop(0, tiles, step=8)
+        left = offs[1, n]
+
+        @pl.loop(0, chips, step=4)
         def _(j0):
-            for dj in range(8):
-                s = lax.rem(XB * (j0 + dj) + 8 * h - left + cols, cols)
-                snd[k, h, j0 + dj] = swap_rows_and_groups(gt[k, pl.ds(s, 8), :])
-
-        mine = pl.ds(pl.multiple_of(CELL * me, CELL), CELL)
-
-        @pl.loop(0, tiles - 1)
+            for dj in range(4):
+                for c in range(2):
+                    s = lax.rem(2 * XB * (j0 + dj) + XB * c + 8 * h - left + cols, cols)
+                    snd[k, h, j0 + dj, c] = swap_rows_and_groups(gt[k, pl.ds(s, 8), :])
+
+        @pl.loop(0, chips - 1)
         def _(i):
-            j = lax.select(lax.rem(i, 2) == 0, i // 2 + 1, tiles - 1 - i // 2)
-            d = lax.rem(me + j, tiles)
+            j = lax.select(lax.rem(i, 2) == 0, i // 2 + 1, chips - 1 - i // 2)
+            d = lax.rem(chip + j, chips)
             pltpu.make_async_remote_copy(
                 src_ref=snd.at[k, h, d],
-                dst_ref=slab[k][h].at[mine, :],
+                dst_ref=land.at[k, h, chip],
                 send_sem=zs.at[k, h],
                 recv_sem=zr.at[k, h],
-                device_id=(n, d),
+                device_id=(n, 2 * d + core),
                 device_id_type=MESH,
             ).start()
 
-        slab[k][h][mine, :] = snd[k, h, me]
+        land[k, h, chip] = snd[k, h, chip]
+
+    def pass_on(k, h):
+        got = land.at[k, h, pl.ds(0, chips - 1)]
+        pltpu.make_async_copy(got, got, zr.at[k, h]).wait()
+        copy = pltpu.make_async_remote_copy(
+            src_ref=land.at[k, h, :, 1 - core],
+            dst_ref=relay.at[k, h],
+            send_sem=fs.at[k, h],
+            recv_sem=fr.at[k, h],
+            device_id=(n, other),
+            device_id_type=MESH,
+        )
+        copy.start()
+        passed[k, h] = copy
 
     def send_nests(k, h):
-        here = slab[k][h]
-        got = here.at[pl.ds(0, rows - CELL), :]
-        pltpu.make_async_copy(got, got, zr.at[k, h]).wait()
-        here[rows : rows + 8, :] = here[0:8, :]
+        passed[k, h].wait()
+        top = offs[0, n]
+
+        @pl.loop(0, chips, step=4)
+        def _(i0):
+            for di in range(4):
+                i = i0 + di
+                slab[pl.ds(pl.multiple_of(16 * i + 8 * core, 8), 8), :] = land[k, h, i, core]
+                slab[pl.ds(pl.multiple_of(16 * i + 8 - 8 * core, 8), 8), :] = relay[k, h, i]
+
+        slab[rows : rows + 8, :] = slab[0:8, :]
 
         @pl.loop(0, rows // 8, step=8)
         def _(g0):
             for dg in range(8):
                 g = g0 + dg
                 s = lax.rem(8 * g - top + rows, rows)
-                half[k, h, pl.ds(pl.multiple_of(8 * g, 8), 8), :] = here[pl.ds(s, 8), :]
+                half[k, h, pl.ds(pl.multiple_of(8 * g, 8), 8), :] = slab[pl.ds(s, 8), :]
 
         for dn in (2, 1, 3):
             b = lax.rem(n + dn, nests)
@@ -201,6 +235,7 @@
                 ].T
 
     def own_rows():
+        small[3].wait()
         for x in range(XB):
             nat[x * FC : (x + 1) * FC, :] = jnp.broadcast_to(prio_ref[x : x + 1, :].astype(f32), (FC, own))
         to_rows(prit)
@@ -219,7 +254,7 @@
     lane = lax.broadcasted_iota(jnp.int32, (8, 128), 1)
     east, west = lax.rem(me + 1, tiles), lax.rem(me + tiles - 1, tiles)
     up, down = lax.rem(n + 1, nests), lax.rem(n + nests - 1, nests)
-    flights, given = {}, []
+    flights, passed, given = {}, {}, []
 
     def merge(k, h):
         got = q.at[k, h, pl.ds(0, nests - 1)]
@@ -300,33 +335,37 @@
             c.start()
             given.append(c)
 
+    small[0].wait()
     spread_row_weights()
     for k in range(chunks):
         compute(k)
         if k == 0:
             for c in taken:
                 c.start()
-            pl.semaphore_wait(barrier, tiles - 1 + nests - 1)
+            for c in small[1:3]:
+                c.wait()
         turn(k)
+        if k == 0:
+            pl.semaphore_wait(barrier, peers)
         for h in range(TILED):
             send_tiles(k, h)
     own_rows()
     order = [(k, h) for k in range(chunks) for h in range(TILED)]
     for i, (k, h) in enumerate(order):
-        send_nests(k, h)
+        pass_on(k, h)
         if i >= 2:
             merge(*order[i - 2])
-            if order[i - 2][1] == TILED - 1 and i < len(order) - 1:
-                finish(order[i - 2][0])
-    for k, h in order[-2:]:
-        if h == 0 and k > 0:
-            finish(k - 1)
+        send_nests(k, h)
+    for i, (k, h) in enumerate(order[-2:]):
+        if i == 0:
+            for done in range(chunks - 1):
+                finish(done)
         merge(k, h)
     finish(chunks - 1)
     for c in given:
         c.wait()
     for k, h in order:
-        sent = slab[k][h].at[pl.ds(0, rows - CELL), :]
+        sent = land.at[k, h, pl.ds(0, chips - 1)]
         pltpu.make_async_copy(sent, sent, zs.at[k, h]).wait()
         sent = q.at[k, h, pl.ds(0, nests - 1)]
         pltpu.make_async_copy(sent, sent, ys.at[k, h]).wait()
@@ -342,16 +381,18 @@
     pieces = min(6, width // 128)
     piece = width // pieces
     packed = own // min(8, own // 8)
-    vm = pl.BlockSpec(memory_space=pltpu.VMEM)
-    sm = pl.BlockSpec(memory_space=pltpu.SMEM)
-    hbm = pl.BlockSpec(memory_space=pl.ANY)
+    hbm = pl.BlockSpec(memory_space=pltpu.HBM)
     dma = pltpu.SemaphoreType.DMA
     return pl.pallas_call(
         kernel,
         out_shape=jax.ShapeDtypeStruct(par.shape, f32),
-        in_specs=[sm, sm, hbm, vm, hbm, vm, hbm],
-        out_specs=hbm,
+        in_specs=[hbm] * 7,
+        out_specs=pl.BlockSpec(memory_space=pl.ANY),
         scratch_shapes=[
+            pltpu.SMEM(offs.shape, jnp.int32),
+            pltpu.SMEM(rate.shape, f32),
+            pltpu.VMEM(row_w.shape, f32),
+            pltpu.VMEM(prio.shape, jnp.int32),
             pltpu.VMEM((chunks, pieces, depth, piece), f32),
             pltpu.VMEM((pieces, piece, cols), f32),
             pltpu.VMEM((pieces, piece, cols), bf16),
@@ -359,8 +400,10 @@
             pltpu.VMEM((2 * FC * CELL, depth), bf16),
             pltpu.VMEM((chunks, FC * CELL, cols), f32),
             pltpu.VMEM((chunks, cols + 8, 128), f32),
-            pltpu.VMEM((chunks, TILED, tiles, CELL, 128), f32),
-            [[pltpu.VMEM((rows + 8, 128), f32) for _ in range(TILED)] for _ in range(chunks)],
+            pltpu.VMEM((chunks, TILED, tiles // 2, 2, CELL, 128), f32),
+            pltpu.VMEM((chunks, TILED, tiles // 2, 2, CELL, 128), f32),
+            pltpu.VMEM((chunks, TILED, tiles // 2, CELL, 128), f32),
+            pltpu.VMEM((rows + 8, 128), f32),
             pltpu.VMEM((chunks, TILED, rows, 128), f32),
             pltpu.VMEM((chunks, TILED, nests, own, 128), f32),
             pltpu.VMEM((chunks, TILED, own + 16, 128), f32),
@@ -372,12 +415,13 @@
             pltpu.VMEM((TILED, own, 128), f32),
             pltpu.VMEM((own // span, par.shape[0], span), f32),
             pltpu.VMEM((own // span, par.shape[0], span), f32),
-            dma((chunks, pieces)), dma((pieces,)), dma((own // span,)), dma((chunks, own // span)),
+            dma((4,)), dma((chunks, pieces)), dma((pieces,)), dma((own // span,)), dma((chunks, own // span)),
             dma((chunks, TILED)), dma((chunks, TILED)), dma((chunks, TILED)), dma((chunks, TILED)),
+            dma((chunks, TILED)), dma((chunks, TILED)),
             dma((chunks, TILED, 4)), dma((chunks, TILED, 4)),
         ],
         compiler_params=pltpu.CompilerParams(
-            collective_id=0, has_side_effects=True, vmem_limit_bytes=60 * 1024 * 1024
+            collective_id=0, has_side_effects=True, vmem_limit_bytes=52 * 1024 * 1024
         ),
     )(offs, rate, child, row_w, col_w, prio, par)
 
@@ -387,7 +431,9 @@
     tiles, nests = lax.axis_size("tile"), lax.axis_size("nest")
     child = child_fields.reshape(-1, child_fields.shape[3])
     par = parent_old.reshape(fields * strip, own)
-    out = feedback(nest_offsets, smooth_rate, child, row_weights, col_weights, priority, par, tiles, nests)
+    args = (nest_offsets.T, smooth_rate, child, row_weights, col_weights, priority, par)
+    args = [pltpu.with_memory_space_constraint(a, pltpu.HBM) for a in args]
+    out = feedback(*args, tiles, nests)
     return out.reshape(fields, strip, own)
 
 

time: 71.5 us -> 64.7 us (0.905)
  Pallas kernels: 67.8 us -> 63.8 us
  local copies, waits for them, and re-layouts: 3.2 us -> 0.8 us
    pallas_call x1, Pallas kernels: 67.8 us -> 63.8 us  [feedback(): pl.pallas_call(kernel, out_shape=jax.ShapeDtypeStruct(par.shape, f32), in...]
    unnamed x2 -> x1, local copies, waits for them, and re-layouts: 3.2 us -> 0.8 us
where the time goes in v3:
time: 64.7 us; the launch traced here: 64.6 us
  Pallas kernels  63.8 us (99%)
  local copies, waits for them, and re-layouts  0.8 us (1%)
    pallas_call x1, Pallas kernels, feedback(): pl.pallas_call(kernel, out_shape=jax.ShapeDtypeStruct(par.shape, f32), in...  63.8 us

profile of v3, /device:TPU:8, one launch (start us, length us, event | category | flops | bytes accessed | tf_op | source)
XLA Modules:
  0.0 64.6 jit_solution(6598801693012447767)
XLA Ops:
  0.0 63.8 %shard_map.73 = f32[512,256]{1,0:T(8,128)S(1)} custom-call(s32[2,4]{1,0:T(2,128)} %bitcast.7, f32[32]{0:T(128)} %rate_in.1, f32[768,3072]{1,0:T(8,128)} %bitcast.5, f32[8,24]{1,0:T(8,128)} %row_in.1, f32[3072,1024]{1,0:T(8,128)} %col_w.1, s32[16,256]{1,0:T(8,128)} %prio_in.1, f32[512,256]{1,0:T(8,128)} %bitcast.6), custom_call_target="tpu_custom_call" | custom-call | tf_op jit(solution)/shard_map/pallas_call | solution.py:386
  63.8 0.8 %copy.9 = f32[32,16,256]{2,1,0:T(8,128)} copy(f32[32,16,256]{2,1,0:T(8,128)S(1)} %bitcast.4) | data formatting | bytes 1048576

commit v4 on v3

--- a/solution.py
+++ b/solution.py
@@ -11,6 +11,7 @@
 XB = 16
 TILED = XB * FC // 128
 AHEAD = 3
+STRIDE = 13
 f32, bf16 = jnp.float32, jnp.bfloat16
 
 
@@ -20,7 +21,7 @@
     for d in (1, 2, 4):
         w = FC * d
         low = pltpu.roll(pltpu.roll(v, CELL - d, 0), w, 1)
-        high = pltpu.roll(pltpu.roll(v, d, 0), 128 - w, 1)
+        high = low if 2 * d == CELL else pltpu.roll(pltpu.roll(v, d, 0), 128 - w, 1)
         sbit, lbit = (sub & d) != 0, (lane & w) != 0
         v = jnp.where(sbit == lbit, v, jnp.where(lbit, low, high))
     return v
@@ -66,7 +67,8 @@
         for i, (a, b) in enumerate(((row_in, row_w), (offs_in, offs), (rate_in, rate), (prio_in, prio_ref)))
     ]
     small[0].start()
-    for c in range(min(AHEAD, pieces)):
+    ahead = next(a for a in range(min(AHEAD, pieces), 0, -1) if pieces % a == 0)
+    for c in range(ahead):
         child_copy(0, c).start()
         weight_copy(c).start()
     for c in small[1:]:
@@ -111,13 +113,16 @@
             if k == 0:
                 weight_copy(c).wait()
 
-                @pl.when(c + AHEAD < pieces)
+                @pl.when(c + ahead < pieces)
                 def _():
-                    child_copy(0, c + AHEAD).start()
-                    weight_copy(c + AHEAD).start()
-
-            if k + 1 < chunks:
-                child_copy(k + 1, c).start()
+                    child_copy(0, c + ahead).start()
+                    weight_copy(c + ahead).start()
+
+                for later in range(1, chunks):
+                    @pl.when(c + ahead >= pieces)
+                    def _():
+                        for i in range(pieces // ahead):
+                            child_copy(later, (c + ahead - pieces) * (pieces // ahead) + i).start()
             left_high, left_low = [], []
             for s in range(piece // step):
                 xh, xl = two_parts(xbuf[k, c, :, s * step : (s + 1) * step])
@@ -148,17 +153,17 @@
     def send_tiles(k, h):
         left = offs[1, n]
 
-        @pl.loop(0, chips, step=4)
+        batch = min(16, chips)
+
+        @pl.loop(0, chips, step=batch)
         def _(j0):
-            for dj in range(4):
+            for dj in range(batch):
                 for c in range(2):
                     s = lax.rem(2 * XB * (j0 + dj) + XB * c + 8 * h - left + cols, cols)
                     snd[k, h, j0 + dj, c] = swap_rows_and_groups(gt[k, pl.ds(s, 8), :])
 
-        @pl.loop(0, chips - 1)
-        def _(i):
-            j = lax.select(lax.rem(i, 2) == 0, i // 2 + 1, chips - 1 - i // 2)
-            d = lax.rem(chip + j, chips)
+        for i in range(chips - 1):
+            d = lax.rem(chip + (i + 1) * STRIDE % chips, chips)
             pltpu.make_async_remote_copy(
                 src_ref=snd.at[k, h, d],
                 dst_ref=land.at[k, h, chip],
@@ -217,10 +222,7 @@
             ).start()
         mine = pl.multiple_of(lax.rem(n * own, rows), own)
 
-        @pl.loop(0, own // 8)
-        def _(g):
-            r = pl.multiple_of(8 * g, 8)
-            q[k, h, n, pl.ds(r, 8), :] = half[k, h, pl.ds(mine + r, 8), :]
+        q[k, h, n] = half[k, h, pl.ds(mine, own), :]
 
     span = min(128, own)
     taken = [
@@ -260,14 +262,12 @@
         got = q.at[k, h, pl.ds(0, nests - 1)]
         pltpu.make_async_copy(got, got, yr.at[k, h]).wait()
 
-        @pl.loop(0, own // 8, step=4)
-        def _(g0):
-            for dg in range(4):
-                r = pl.ds(pl.multiple_of(8 * (g0 + dg), 8), 8)
-                v, p = part[k, h, r, :], prit[h, r, :]
-                for m in range(nests):
-                    v = jnp.where(p == float(m), q[k, h, m, r, :], v)
-                mrg[k, h, pl.ds(pl.multiple_of(8 * (g0 + dg) + 8, 8), 8), :] = v
+        for g in range(own // 8):
+            r = slice(8 * g, 8 * g + 8)
+            v, p = part[k, h, r, :], prit[h, r, :]
+            for m in range(nests):
+                v = jnp.where(p == float(m), q[k, h, m, r, :], v)
+            mrg[k, h, 8 * g + 8 : 8 * g + 16, :] = v
 
         moves = [
             (mrg.at[k, h, pl.ds(8, 8), :], mrg.at[k, h, pl.ds(own + 8, 8), :], (down, me)),
@@ -306,11 +306,10 @@
             r = jnp.where(lax.rem(lane, FC) == f, rate[k * FC + f], r)
 
         for j in range(packs):
-            @pl.loop(0, packed // 8)
-            def _(i):
-                o = pl.multiple_of(packed * j + 8 * i, 8)
-                e = halo[k, 0, pl.ds(pl.multiple_of(8 * i, 8), 8), :]
-                w = halo[k, 1, pl.ds(pl.multiple_of(8 * i, 8), 8), :]
+            for i in range(packed // 8):
+                o = packed * j + 8 * i
+                e = halo[k, 0, 8 * i : 8 * i + 8, :]
+                w = halo[k, 1, 8 * i : 8 * i + 8, :]
                 es, ws_ = (128 - FC - FC * j) % 128, (128 - FC * j) % 128
                 e = pltpu.roll(e, es, 1) if es else e
                 w = pltpu.roll(w, ws_, 1) if ws_ else w
@@ -347,15 +346,23 @@
         turn(k)
         if k == 0:
             pl.semaphore_wait(barrier, peers)
+        if k:
+            pass_on(k - 1, 0)
         for h in range(TILED):
             send_tiles(k, h)
+            if k and h == 0:
+                send_nests(k - 1, 0)
     own_rows()
     order = [(k, h) for k in range(chunks) for h in range(TILED)]
-    for i, (k, h) in enumerate(order):
-        pass_on(k, h)
-        if i >= 2:
-            merge(*order[i - 2])
-        send_nests(k, h)
+    waiting = []
+    for k, h in order:
+        if (k, h) not in passed:
+            pass_on(k, h)
+        if len(waiting) > 1:
+            merge(*waiting.pop(0))
+        if h or k == chunks - 1:
+            send_nests(k, h)
+        waiting.append((k, h))
     for i, (k, h) in enumerate(order[-2:]):
         if i == 0:
             for done in range(chunks - 1):

time: 64.7 us -> 58.1 us (0.90); the launches traced: 64.6 us -> 57.3 us
  Pallas kernels: 63.8 us -> 56.5 us
    pallas_call x1, Pallas kernels: 63.8 us -> 56.5 us  [feedback(): pl.pallas_call(kernel, out_shape=jax.ShapeDtypeStruct(par.shape, f32), in...]
where the time goes in v4:
time: 58.1 us; the launch traced here: 57.3 us
  Pallas kernels  56.5 us (97%)
  local copies, waits for them, and re-layouts  0.8 us (1%)
    pallas_call x1, Pallas kernels, feedback(): pl.pallas_call(kernel, out_shape=jax.ShapeDtypeStruct(par.shape, f32), in...  56.5 us

profile of v4, /device:TPU:8, one launch (start us, length us, event | category | flops | bytes accessed | tf_op | source)
XLA Modules:
  0.0 57.3 jit_solution(16309550672638237958)
XLA Ops:
  0.0 56.5 %shard_map.73 = f32[512,256]{1,0:T(8,128)S(1)} custom-call(s32[2,4]{1,0:T(2,128)} %bitcast.7, f32[32]{0:T(128)} %rate_in.1, f32[768,3072]{1,0:T(8,128)} %bitcast.5, f32[8,24]{1,0:T(8,128)} %row_in.1, f32[3072,1024]{1,0:T(8,128)} %col_w.1, s32[16,256]{1,0:T(8,128)} %prio_in.1, f32[512,256]{1,0:T(8,128)} %bitcast.6), custom_call_target="tpu_custom_call" | custom-call | tf_op jit(solution)/shard_map/pallas_call | solution.py:393
  56.5 0.8 %copy.9 = f32[32,16,256]{2,1,0:T(8,128)} copy(f32[32,16,256]{2,1,0:T(8,128)S(1)} %bitcast.4) | data formatting | bytes 1048576

commit v5 on v4

--- a/solution.py
+++ b/solution.py
@@ -77,8 +77,7 @@
     barrier = pltpu.get_barrier_semaphore()
     peers = chips - 1 + nests - 1 + 2
 
-    @pl.loop(1, chips)
-    def _(j):
+    for j in range(1, chips):
         d = 2 * lax.rem(chip + j, chips) + core
         pl.semaphore_signal(barrier, inc=1, device_id=(n, d), device_id_type=MESH)
 
@@ -190,26 +189,31 @@
         passed[k, h] = copy
 
     def send_nests(k, h):
+        top = offs[0, n]
+        for i in range(chips):
+            slab[pl.ds(pl.multiple_of(16 * i + 8 * core, 8), 8), :] = land[k, h, i, core]
         passed[k, h].wait()
-        top = offs[0, n]
-
-        @pl.loop(0, chips, step=4)
-        def _(i0):
-            for di in range(4):
-                i = i0 + di
-                slab[pl.ds(pl.multiple_of(16 * i + 8 * core, 8), 8), :] = land[k, h, i, core]
-                slab[pl.ds(pl.multiple_of(16 * i + 8 - 8 * core, 8), 8), :] = relay[k, h, i]
+        for i in range(chips):
+            slab[pl.ds(pl.multiple_of(16 * i + 8 - 8 * core, 8), 8), :] = relay[k, h, i]
 
         slab[rows : rows + 8, :] = slab[0:8, :]
 
-        @pl.loop(0, rows // 8, step=8)
-        def _(g0):
-            for dg in range(8):
-                g = g0 + dg
-                s = lax.rem(8 * g - top + rows, rows)
-                half[k, h, pl.ds(pl.multiple_of(8 * g, 8), 8), :] = slab[pl.ds(s, 8), :]
-
+        batch = min(16, own // 8)
+
+        def turn_rows(c0):
+            @pl.loop(0, own // 8, step=batch)
+            def _(g0):
+                for dg in range(batch):
+                    r = c0 + 8 * (g0 + dg)
+                    s = lax.rem(r - top + rows, rows)
+                    half[k, h, pl.ds(pl.multiple_of(r, 8), 8), :] = slab[pl.ds(s, 8), :]
+
+        here = pl.multiple_of(lax.rem(n * own, rows), own)
+        away = pl.multiple_of(lax.rem((n + 1) * own, rows), own)
+        turn_rows(here)
         for dn in (2, 1, 3):
+            if dn == 1:
+                turn_rows(away)
             b = lax.rem(n + dn, nests)
             start = pl.multiple_of(lax.rem(b * own, rows), own)
             pltpu.make_async_remote_copy(

time: 58.1 us -> 57.8 us (level)
  no operation moved by 1% of the time
where the time goes in v5:
time: 57.8 us; the launch traced here: 57.3 us
  Pallas kernels  56.5 us (98%)
  local copies, waits for them, and re-layouts  0.8 us (1%)
    pallas_call x1, Pallas kernels, feedback(): pl.pallas_call(kernel, out_shape=jax.ShapeDtypeStruct(par.shape, f32), in...  56.5 us

profile of v5, /device:TPU:8, one launch (start us, length us, event | category | flops | bytes accessed | tf_op | source)
XLA Modules:
  0.0 57.3 jit_solution(16763214501177913116)
XLA Ops:
  0.0 56.5 %shard_map.73 = f32[512,256]{1,0:T(8,128)S(1)} custom-call(s32[2,4]{1,0:T(2,128)} %bitcast.7, f32[32]{0:T(128)} %rate_in.1, f32[768,3072]{1,0:T(8,128)} %bitcast.5, f32[8,24]{1,0:T(8,128)} %row_in.1, f32[3072,1024]{1,0:T(8,128)} %col_w.1, s32[16,256]{1,0:T(8,128)} %prio_in.1, f32[512,256]{1,0:T(8,128)} %bitcast.6), custom_call_target="tpu_custom_call" | custom-call | tf_op jit(solution)/shard_map/pallas_call | solution.py:397
  56.5 0.8 %copy.9 = f32[32,16,256]{2,1,0:T(8,128)} copy(f32[32,16,256]{2,1,0:T(8,128)S(1)} %bitcast.4) | data formatting | bytes 1048576
